TPU v7x, 32 devices: a whole 2x2x4 slice. The times are simulated.
32 devices in a mesh: rep: 4 (over z), own: 8 (over y, x, core).
Axes of the slice: x: 2, y: 2, z: 4, core: 2. Of those that a mesh axis runs over, the one named last changes fastest.
Arguments:
- grads: float32 [16, 576, 1024], P('rep', 'own'), may hold values from -60 to 60
- momentum: bfloat16 [32, 576, 1024], P(('rep', 'own')), may hold values from -6 to 6
- owner_table: int32 [4, 8], replicated, may hold values from 0 to 7, each once within a row
Outputs:
- new_momentum: bfloat16 [32, 576, 1024], P(('rep', 'own'))
- updates: bfloat16 [16, 576, 1024], P(None, 'own')
Inputs may be any that keep to these rules, and one draw needn't show every extreme that they name: Each row of owner_table is a permutation of 0 to 7; entries of 4 or more mark empty slots.
All inputs are finite; a program needn't handle non-finite values.
Results may differ from a plain program's by a relative error of at most 0.01.
Values may be sent and summed in bfloat16 or wider, within the bound.
No kernel may reach another device: no remote copies, remote signals or barrier semaphores. Data moves between devices by JAX's collectives and lax.ppermute only.
A program may use at most 128 MiB of HBM per device.

v0:
```python
import math
import jax
import jax.numpy as jnp
from jax import lax
from jax.sharding import PartitionSpec as P

ITERS = 2
DECAY = 0.95
COEF_A = 3.4445
COEF_B = -4.775
COEF_C = 2.0315
EPSILON = 1e-07


def orthogonalize(blend):
    total = jnp.sqrt(jnp.sum(blend * blend))
    iterate = (blend / (total + EPSILON)).astype(jnp.bfloat16)
    factor = 0.2 * math.sqrt(max(blend.shape[0], blend.shape[1]))
    result = None
    for turn in range(ITERS):
        gram = jnp.dot(iterate, iterate.T, preferred_element_type=jnp.float32).astype(jnp.bfloat16)
        square = jnp.dot(gram, gram, preferred_element_type=jnp.float32)
        poly = (COEF_B * gram.astype(jnp.float32) + COEF_C * square).astype(jnp.bfloat16)
        mixed = COEF_A * iterate.astype(jnp.float32) + jnp.dot(
            poly, iterate, preferred_element_type=jnp.float32
        )
        if turn + 1 < ITERS:
            iterate = mixed.astype(jnp.bfloat16)
        else:
            result = (factor * mixed).astype(jnp.bfloat16)
    return result


def body(grads, momentum, owner_table):
    group = lax.axis_index("rep")
    slot_matrix = lax.dynamic_index_in_dim(owner_table, group, 0, keepdims=False)
    matrix_count, shard_rows, columns = grads.shape
    is_live = slot_matrix < matrix_count
    clamped = jnp.minimum(slot_matrix, matrix_count - 1)
    half_grads = grads.astype(jnp.bfloat16)
    outgoing = jnp.take(half_grads, clamped, axis=0) * is_live[:, None, None].astype(jnp.bfloat16)
    incoming = lax.all_to_all(outgoing, "own", split_axis=0, concat_axis=1, tiled=True)
    gradient = incoming[0].astype(jnp.float32)
    moment = DECAY * momentum[0].astype(jnp.float32) + gradient
    new_momentum = moment.astype(jnp.bfloat16)[None]
    update = orthogonalize(gradient + DECAY * moment)
    returned = lax.all_to_all(update[None], "own", split_axis=1, concat_axis=0, tiled=True)
    holders = jnp.argsort(slot_matrix)[:matrix_count]
    grouped = jnp.take(returned, holders, axis=0)
    updates = lax.all_gather(grouped, "rep", axis=0, tiled=True)
    return (new_momentum, updates)


def solution(mesh):
    in_specs = (P("rep", "own", None), P(("rep", "own"), None, None), P())
    out_specs = (P(("rep", "own"), None, None), P(None, "own", None))
    return jax.shard_map(body, mesh=mesh, in_specs=in_specs, out_specs=out_specs, check_vma=False)
```

profile of v0, /device:TPU:0, one launch (start us, length us, event | category | flops | bytes accessed | tf_op | source)
XLA Modules:
  0.0 138.9 jit_solution(14850939103805925869)
XLA Ops:
  7.2 0.7 compare_convert_fusion
  7.9 0.7 fusion.10
  8.6 1.4 convert_element_type.90
  9.9 0.6 gather_fusion
  10.8 21.7 %all_to_all.21 = bf16[8,72,1024]{2,1,0:T(8,128)(2,1)S(1)} all-to-all(bf16[8,72,1024]{2,1,0:T(8,128)(2,1)S(1)} %select_multiply_fusion), channel_id=1, replica_groups=mesh['rep'=4,'own'=8] {'own'}, dimensions={0} | all-to-all | bytes 2359296 | tf_op jit(solution)/shard_map/all_to_all | solution.py:42
  32.8 1.0 copy-done
  33.8 1.5 %convert_multiply_fusion = (f32[1,576,1024]{2,1,0:T(8,128)S(1)}, bf16[1,576,1024]{2,1,0:T(8,128)(2,1)}) fusion(bf16[1,576,1024]{2,1,0:T(8,128)(2,1)S(1)} %copy-done, f32[1,576,1024]{2,1,0:T(8,128)S(1)} %bitcast.46), kind=kLoop, calls=%fused_computation.13 | loop fusion | flops 2359296 | bytes 7077888 | tf_op jit(solution)/shard_map/mul | solution.py:44
  35.3 1.2 multiply_reduce_fusion
  37.7 1.1 convolution_convert_fusion.1
  39.0 0.6 fusion.4
  39.6 1.7 %add_convert_fusion = bf16[576,1024]{1,0:T(8,128)(2,1)S(1)} fusion(bf16[576,1024]{1,0:T(8,128)(2,1)S(1)} %fusion.4, bf16[576,576]{1,0:T(8,128)(2,1)S(1)} %convolution_convert_fusion.1), kind=kOutput, calls=%fused_computation.9 | convolution fusion | flops 1065701376 | bytes 3022848 | tf_op jit(solution)/shard_map/dot_general | solution.py:24
  41.3 1.1 convolution_convert_fusion
  42.4 1.7 %fusion.5 = bf16[1,576,1024]{2,1,0:T(8,128)(2,1)S(1)} fusion(bf16[576,1024]{1,0:T(8,128)(2,1)S(1)} %add_convert_fusion, bf16[576,576]{1,0:T(8,128)(2,1)S(1)} %convolution_convert_fusion), kind=kOutput, calls=%fused_computation.17 | convolution fusion | flops 1066291200 | bytes 3022848 | tf_op jit(solution)/shard_map/dot_general | solution.py:24
  44.1 1.8 %copy.9 = bf16[1,576,1024]{2,0,1:T(2,128)(2,1)S(1)} copy(bf16[1,576,1024]{2,1,0:T(8,128)(2,1)S(1)} %fusion.5) | data formatting | bytes 2359296 | tf_op jit(solution)/shard_map/broadcast_in_dim | solution.py:47
  46.5 7.7 %reduce.3 = bf16[576,1024]{1,0:T(8,128)(2,1)S(1)} reduce(bf16[576,1,1024]{2,1,0:T(2,128)(2,1)S(1)} %bitcast.47, bf16[]{:T(256)} %broadcast.140), dimensions={1}, to_apply=%bitcast.43.reduce_sub_computation | reduce | bytes 2359298
  54.2 1.6 %reshape.107 = bf16[8,2,36864]{2,1,0:T(2,128)(2,1)} reshape(bf16[576,1024]{1,0:T(8,128)(2,1)S(1)} %reduce.3) | data formatting | bytes 2359296
  55.8 3.6 %all-to-all-start.1 = ((bf16[8,2,36864]{2,1,0:T(2,128)(2,1)}), bf16[8,2,36864]{2,1,0:T(2,128)(2,1)S(1)}, u32[]{:S(2)}, u32[]{:S(2)}) async-start(bf16[8,2,36864]{2,1,0:T(2,128)(2,1)} %reshape.107), calls=%async_computation.1 | async-start | bytes 2359296 | tf_op jit(solution)/shard_map/all_to_all | solution.py:47
  59.4 1.0 sort.17
  60.5 15.6 %all-to-all-done.1 = bf16[8,2,36864]{2,1,0:T(2,128)(2,1)S(1)} async-done(((bf16[8,2,36864]{2,1,0:T(2,128)(2,1)}), bf16[8,2,36864]{2,1,0:T(2,128)(2,1)S(1)}, u32[]{:S(2)}, u32[]{:S(2)}) %all-to-all-start.1) | async-done | bytes 1179680 | tf_op jit(solution)/shard_map/all_to_all | solution.py:47
  76.1 1.1 reshape.108
  77.7 0.6 gather_fusion.1
  78.3 0.9 broadcast_select_fusion
  79.2 49.5 %all-gather.2.cloned.1.call-done = bf16[16,72,1024]{2,1,0:T(8,128)(2,1)} async-done(((bf16[4,72,1024]{2,1,0:T(8,128)(2,1)}), bf16[16,72,1024]{2,1,0:T(8,128)(2,1)}) %all-gather.2.cloned.1.call-update) | async-done | bytes 2359312 | tf_op jit(solution)/shard_map/all_gather | solution.py:50
  128.8 3.3 %copy.11 = bf16[16,72,1024]{2,1,0:T(8,128)(2,1)} copy(bf16[16,72,1024]{2,1,0:T(8,128)(2,1)} %all-gather.2.cloned.1.call-done) | data formatting | bytes 4718592
  (15 shorter events, 2.1 us)
Async XLA Ops:
  32.5 1.3 copy-start
  37.7 1.3 copy-start.1
  55.8 20.3 %all-to-all-start.1 = ((bf16[8,2,36864]{2,1,0:T(2,128)(2,1)}), bf16[8,2,36864]{2,1,0:T(2,128)(2,1)S(1)}, u32[]{:S(2)}, u32[]{:S(2)}) async-start(bf16[8,2,36864]{2,1,0:T(2,128)(2,1)} %reshape.107), calls=%async_computation.1 | async-start | bytes 2359296 | tf_op jit(solution)/shard_map/all_to_all | solution.py:47
  59.4 69.4 %all-gather.2.cloned.1.call-start = ((), (), s32[]{:S(2)}) async-start(), calls=%async_computation.2 | async-start | bytes 2949120 | tf_op jit(solution)/shard_map/all_gather | solution.py:50
Sparse Core Ops, SparseCore 0:
  79.4 49.3 all-gather.1
where the time goes:
time: 139 us
  waiting for transfers between devices  65.1 us (47%)
  blocking collectives  21.7 us (16%)
  other arithmetic  16.7 us (12%)
  between operations  14.9 us (11%)
  local copies, waits for them, and re-layouts  11.1 us (8%)
  matrix products  5.68 us (4%)
  starting transfers between devices  3.61 us (3%)
    all_gather x1, waiting for transfers between devices, body(): updates = lax.all_gather(grouped, 'rep', axis=0, tiled=True)  49.5 us
    all_to_all x1, blocking collectives, body(): lax.all_to_all(outgoing, 'own', split_axis=0, concat_axis=1, tiled=True)  21.7 us
    all_to_all x1, waiting for transfers between devices, body(): lax.all_to_all(update[None], 'own', split_axis=1, concat_axis=0, tiled=True)  15.6 us
    unnamed x9, local copies, waits for them, and re-layouts  8.11 us
    unnamed x1, other arithmetic  7.72 us
    all_to_all x1, starting transfers between devices, body(): lax.all_to_all(update[None], 'own', split_axis=1, concat_axis=0, tiled=True)  3.56 us
    dot_general x2, matrix products, orthogonalize(): jnp.dot(poly, iterate, preferred_element_type=jnp.float32)  3.45 us
  transfers between devices with their start and end apart: 2, of which 2 were waited for; matrix products, arithmetic and copies ran while one was open for 1% of the time, Pallas kernels for 0%

commit v1 on v0

--- a/solution.py
+++ b/solution.py
@@ -10,6 +10,22 @@
 COEF_B = -4.775
 COEF_C = 2.0315
 EPSILON = 1e-07
+
+
+def order_limits(xin, a_name, dim_no):
+    q_n = lax.psum(1, axis_name=a_name)
+    pages = []
+    for dev in range(1, q_n):
+        pages.append((dev - 1, dev))
+    a_now = pages + [(q_n - 1, 0)]
+    m_next = xin
+    steps_seen = [m_next]
+    for _ in range(q_n - 1):
+        m_next = lax.ppermute(m_next, axis_name=a_name, perm=a_now)
+        steps_seen += [m_next]
+    top = jnp.concatenate([*reversed(steps_seen)], dim_no)
+    r1 = jnp.roll(top, (lax.axis_index(a_name) + 1) * m_next.shape[dim_no], axis=dim_no)
+    return r1
 
 
 def orthogonalize(blend):
@@ -47,7 +63,7 @@
     returned = lax.all_to_all(update[None], "own", split_axis=1, concat_axis=0, tiled=True)
     holders = jnp.argsort(slot_matrix)[:matrix_count]
     grouped = jnp.take(returned, holders, axis=0)
-    updates = lax.all_gather(grouped, "rep", axis=0, tiled=True)
+    updates = order_limits(grouped, "rep", 0)
     return (new_momentum, updates)
 
 

time: 139 us -> 121 us (0.87)
  waiting for transfers between devices: 65.1 us -> 45.8 us
  blocking collectives: 21.7 us -> 40.9 us
  between operations: 14.9 us -> 1.53 us
  local copies, waits for them, and re-layouts: 11.1 us -> 8.91 us
  starting transfers between devices: 3.61 us -> 1.64 us
    all_gather x1 -> x0, waiting for transfers between devices: 49.5 us -> none  [body(): updates = lax.all_gather(grouped, 'rep', axis=0, tiled=True)]
    ppermute x0 -> x3, waiting for transfers between devices: none -> 45.8 us  [order_limits(): m_next = lax.ppermute(m_next, axis_name=a_name, perm=a_now)]
    all_to_all x0 -> x1, blocking collectives: none -> 19.1 us  [body(): lax.all_to_all(update[None], 'own', split_axis=1, concat_axis=0, tiled=True)]
    all_to_all x1 -> x0, waiting for transfers between devices: 15.6 us -> none  [body(): lax.all_to_all(update[None], 'own', split_axis=1, concat_axis=0, tiled=True)]
    unnamed x9 -> x14, local copies, waits for them, and re-layouts: 8.11 us -> 4.26 us
    all_to_all x1 -> x0, starting transfers between devices: 3.56 us -> none  [body(): lax.all_to_all(update[None], 'own', split_axis=1, concat_axis=0, tiled=True)]
    ppermute x0 -> x3, starting transfers between devices: none -> 1.64 us  [order_limits(): m_next = lax.ppermute(m_next, axis_name=a_name, perm=a_now)]
    dynamic_slice x0 -> x1, local copies, waits for them, and re-layouts: none -> 1.62 us  [order_limits(): jnp.roll(top, (lax.axis_index(a_name) + 1) * m_next.shape[dim_no], axis=d...]
  transfers between devices with their start and end apart: 2 -> 3, of which waited for: 2 -> 3; matrix products, arithmetic and copies ran while one was open for 1% -> 0% of each run, Pallas kernels for 0% -> 0%
where the time goes in v1:
time: 121 us
  waiting for transfers between devices  45.8 us (38%)
  blocking collectives  40.9 us (34%)
  other arithmetic  16.2 us (13%)
  local copies, waits for them, and re-layouts  8.91 us (7%)
  matrix products  5.68 us (5%)
  starting transfers between devices  1.64 us (1%)
  between operations  1.53 us (1%)
    ppermute x3, waiting for transfers between devices, order_limits(): m_next = lax.ppermute(m_next, axis_name=a_name, perm=a_now)  45.8 us
    all_to_all x1, blocking collectives, body(): lax.all_to_all(outgoing, 'own', split_axis=0, concat_axis=1, tiled=True)  21.7 us
    all_to_all x1, blocking collectives, body(): lax.all_to_all(update[None], 'own', split_axis=1, concat_axis=0, tiled=True)  19.1 us
    unnamed x2, other arithmetic  7.91 us
    unnamed x14, local copies, waits for them, and re-layouts  4.26 us
    dot_general x2, matrix products, orthogonalize(): jnp.dot(poly, iterate, preferred_element_type=jnp.float32)  3.45 us
  transfers between devices with their start and end apart: 3, of which 3 were waited for; matrix products, arithmetic and copies ran while one was open for 0% of the time, Pallas kernels for 0%

profile of v1, /device:TPU:0, one launch (start us, length us, event | category | flops | bytes accessed | tf_op | source)
XLA Modules:
  0.0 120.6 jit_solution(4126468157628201671)
XLA Ops:
  0.6 0.7 fusion.10
  1.3 0.7 compare_convert_fusion
  2.0 1.0 sort.17
  3.0 1.4 %convert_element_type.90 = bf16[4,72,1024]{2,1,0:T(8,128)(2,1)S(1)} convert(f32[4,72,1024]{2,1,0:T(8,128)} %param.3) | non-fusion elementwise | flops 294912 | bytes 1769472 | tf_op jit(solution)/shard_map/convert_element_type | solution.py:56
  4.4 0.6 gather_fusion
  5.2 21.7 %all_to_all.21 = bf16[8,72,1024]{2,1,0:T(8,128)(2,1)S(1)} all-to-all(bf16[8,72,1024]{2,1,0:T(8,128)(2,1)S(1)} %select_multiply_fusion), channel_id=1, replica_groups=mesh['rep'=4,'own'=8] {'own'}, dimensions={0} | all-to-all | bytes 2359296 | tf_op jit(solution)/shard_map/all_to_all | solution.py:58
  27.2 1.0 copy-done
  28.2 1.5 %convert_multiply_fusion = (f32[1,576,1024]{2,1,0:T(8,128)S(1)}, bf16[1,576,1024]{2,1,0:T(8,128)(2,1)}) fusion(bf16[1,576,1024]{2,1,0:T(8,128)(2,1)S(1)} %copy-done, f32[1,576,1024]{2,1,0:T(8,128)S(1)} %bitcast.46), kind=kLoop, calls=%fused_computation.13 | loop fusion | flops 2359296 | bytes 7077888 | tf_op jit(solution)/shard_map/mul | solution.py:60
  29.7 1.2 %multiply_reduce_fusion = f32[]{:T(128)} fusion(f32[8,72,1024]{2,1,0:T(8,128)S(1)} %bitcast.44, bf16[8,72,1024]{2,1,0:T(8,128)(2,1)S(1)} %all_to_all.21), kind=kLoop, calls=%fused_computation.11 | loop fusion | flops 3538943 | bytes 3538948 | tf_op jit(solution)/shard_map/reduce_sum | solution.py:32
  32.1 1.1 convolution_convert_fusion.1
  33.4 0.6 fusion.4
  34.0 1.7 %add_convert_fusion = bf16[576,1024]{1,0:T(8,128)(2,1)S(1)} fusion(bf16[576,1024]{1,0:T(8,128)(2,1)S(1)} %fusion.4, bf16[576,576]{1,0:T(8,128)(2,1)S(1)} %convolution_convert_fusion.1), kind=kOutput, calls=%fused_computation.9 | convolution fusion | flops 1065701376 | bytes 3022848 | tf_op jit(solution)/shard_map/dot_general | solution.py:40
  35.7 1.1 convolution_convert_fusion
  36.8 1.7 %fusion.5 = bf16[1,576,1024]{2,1,0:T(8,128)(2,1)S(1)} fusion(bf16[576,1024]{1,0:T(8,128)(2,1)S(1)} %add_convert_fusion, bf16[576,576]{1,0:T(8,128)(2,1)S(1)} %convolution_convert_fusion), kind=kOutput, calls=%fused_computation.17 | convolution fusion | flops 1066291200 | bytes 3022848 | tf_op jit(solution)/shard_map/dot_general | solution.py:40
  38.6 1.8 %copy.9 = bf16[1,576,1024]{2,0,1:T(2,128)(2,1)S(1)} copy(bf16[1,576,1024]{2,1,0:T(8,128)(2,1)S(1)} %fusion.5) | data formatting | bytes 2359296 | tf_op jit(solution)/shard_map/broadcast_in_dim | solution.py:63
  40.9 7.7 %reduce.3 = bf16[576,1024]{1,0:T(8,128)(2,1)S(1)} reduce(bf16[576,1,1024]{2,1,0:T(2,128)(2,1)S(1)} %bitcast.47, bf16[]{:T(256)} %broadcast.141), dimensions={1}, to_apply=%bitcast.43.reduce_sub_computation | reduce | bytes 2359298
  48.7 0.8 reshape.107
  49.5 19.1 %all_to_all.22 = bf16[8,2,36864]{2,1,0:T(2,128)(2,1)S(1)} all-to-all(bf16[8,2,36864]{2,1,0:T(2,128)(2,1)S(1)} %reshape.107), channel_id=1, replica_groups=mesh['rep'=4,'own'=8] {'own'}, dimensions={0} | all-to-all | bytes 2359296 | tf_op jit(solution)/shard_map/all_to_all | solution.py:63
  68.6 1.1 reshape.108
  70.9 1.6 %collective-permute-start = (bf16[4,72,1024]{2,1,0:T(8,128)(2,1)S(1)}, bf16[4,72,1024]{2,1,0:T(8,128)(2,1)S(1)}, u32[]{:S(2)}, u32[]{:S(2)}) collective-permute-start(bf16[4,72,1024]{2,1,0:T(8,128)(2,1)S(1)} %broadcast_select_fusion), channel_id=1, source_target_pairs={{0,8},{8,16},{16,24},{24,0},{1,9},{9,17},{17,25},{25,1},{2,10},{10... | collective-permute-start | bytes 1769480 | tf_op jit(solution)/shard_map/ppermute | solution.py:24
  72.5 15.1 %collective-permute-done = bf16[4,72,1024]{2,1,0:T(8,128)(2,1)S(1)} collective-permute-done((bf16[4,72,1024]{2,1,0:T(8,128)(2,1)S(1)}, bf16[4,72,1024]{2,1,0:T(8,128)(2,1)S(1)}, u32[]{:S(2)}, u32[]{:S(2)}) %collective-permute-start) | collective-permute-done | bytes 589856 | tf_op jit(solution)/shard_map/ppermute | solution.py:24
  87.6 15.8 %collective-permute-done.1 = bf16[4,72,1024]{2,1,0:T(8,128)(2,1)S(1)} collective-permute-done((bf16[4,72,1024]{2,1,0:T(8,128)(2,1)S(1)}, bf16[4,72,1024]{2,1,0:T(8,128)(2,1)S(1)}, u32[]{:S(2)}, u32[]{:S(2)}) %collective-permute-start.1) | collective-permute-done | bytes 589856 | tf_op jit(solution)/shard_map/ppermute | solution.py:24
  103.4 14.9 %collective-permute-done.2 = bf16[4,72,1024]{2,1,0:T(8,128)(2,1)S(1)} collective-permute-done((bf16[4,72,1024]{2,1,0:T(8,128)(2,1)S(1)}, bf16[4,72,1024]{2,1,0:T(8,128)(2,1)S(1)}, u32[]{:S(2)}, u32[]{:S(2)}) %collective-permute-start.2) | collective-permute-done | bytes 589856 | tf_op jit(solution)/shard_map/ppermute | solution.py:24
  119.0 1.6 %constant_dynamic-slice_fusion = bf16[16,72,1024]{2,1,0:T(8,128)(2,1)} fusion(bf16[32,72,1024]{2,1,0:T(8,128)(2,1)S(1)} %constant_dynamic-update-slice_fusion, s32[]{:T(128)S(6)} %select_n.53), kind=kLoop, calls=%fused_computation.43 | loop fusion | bytes 4718596 | tf_op jit(solution)/shard_map/jit(_roll_dynamic)/dynamic_slice | solution.py:27
  (24 shorter events, 3.4 us)
Async XLA Ops:
  26.9 1.3 %copy-start = (bf16[1,576,1024]{2,1,0:T(8,128)(2,1)S(1)}, bf16[1,576,1024]{2,1,0:T(8,128)(2,1)}, u32[]{:S(2)}) copy-start(bf16[1,576,1024]{2,1,0:T(8,128)(2,1)} %param.4) | copy-start | bytes 3538948
  32.1 1.3 %copy-start.1 = (bf16[1,576,1024]{2,1,0:T(8,128)(2,1)S(1)}, bf16[1,576,1024]{2,1,0:T(8,128)(2,1)}, u32[]{:S(2)}) copy-start(bf16[1,576,1024]{2,1,0:T(8,128)(2,1)} %param.4) | copy-start | bytes 3538948
  70.9 16.7 %collective-permute-start = (bf16[4,72,1024]{2,1,0:T(8,128)(2,1)S(1)}, bf16[4,72,1024]{2,1,0:T(8,128)(2,1)S(1)}, u32[]{:S(2)}, u32[]{:S(2)}) collective-permute-start(bf16[4,72,1024]{2,1,0:T(8,128)(2,1)S(1)} %broadcast_select_fusion), channel_id=1, source_target_pairs={{0,8},{8,16},{16,24},{24,0},{1,9},{9,17},{17,25},{25,1},{2,10},{10... | collective-permute-start | bytes 1769480 | tf_op jit(solution)/shard_map/ppermute | solution.py:24
  87.6 15.8 %collective-permute-start.1 = (bf16[4,72,1024]{2,1,0:T(8,128)(2,1)S(1)}, bf16[4,72,1024]{2,1,0:T(8,128)(2,1)S(1)}, u32[]{:S(2)}, u32[]{:S(2)}) collective-permute-start(bf16[4,72,1024]{2,1,0:T(8,128)(2,1)S(1)} %collective-permute-done), channel_id=1, source_target_pairs={{0,8},{8,16},{16,24},{24,0},{1,9},{9,17},{17,25},{25,1},{2,10},{10... | collective-permute-start | bytes 1769480 | tf_op jit(solution)/shard_map/ppermute | solution.py:24
  103.4 14.9 %collective-permute-start.2 = (bf16[4,72,1024]{2,1,0:T(8,128)(2,1)S(1)}, bf16[4,72,1024]{2,1,0:T(8,128)(2,1)S(1)}, u32[]{:S(2)}, u32[]{:S(2)}) collective-permute-start(bf16[4,72,1024]{2,1,0:T(8,128)(2,1)S(1)} %collective-permute-done.1), channel_id=1, source_target_pairs={{0,8},{8,16},{16,24},{24,0},{1,9},{9,17},{17,25},{25,1},{2,10},{10... | collective-permute-start | bytes 1769480 | tf_op jit(solution)/shard_map/ppermute | solution.py:24

commit v2 on v0

--- a/solution.py
+++ b/solution.py
@@ -3,6 +3,7 @@
 import jax.numpy as jnp
 from jax import lax
 from jax.sharding import PartitionSpec as P
+from jax.lax import all_to_all, axis_size
 
 ITERS = 2
 DECAY = 0.95
@@ -44,7 +45,15 @@
     moment = DECAY * momentum[0].astype(jnp.float32) + gradient
     new_momentum = moment.astype(jnp.bfloat16)[None]
     update = orthogonalize(gradient + DECAY * moment)
-    returned = lax.all_to_all(update[None], "own", split_axis=1, concat_axis=0, tiled=True)
+
+    def lanes_detail(view, along_dim, which_dim=0):
+        met_up = all_to_all(
+            jnp.stack(jnp.split(view, axis_size("own"), axis=along_dim)), "own", 0, 0
+        )
+        local_next = jnp.concatenate(met_up, axis=which_dim)
+        return local_next
+
+    returned = lanes_detail(update[None], 1)
     holders = jnp.argsort(slot_matrix)[:matrix_count]
     grouped = jnp.take(returned, holders, axis=0)
     updates = lax.all_gather(grouped, "rep", axis=0, tiled=True)

time: 139 us -> 134 us (0.964)
  other arithmetic: 16.7 us -> 9.06 us
  matrix products: 5.68 us -> 8.51 us
    unnamed x1 -> x0, other arithmetic: 7.72 us -> none
    dot_general x2, matrix products: 3.45 us -> 5.42 us  [orthogonalize(): jnp.dot(poly, iterate, preferred_element_type=jnp.float32)]
    broadcast_in_dim x1 -> x0, local copies, waits for them, and re-layouts: 1.82 us -> none  [body(): update[None]]
    unnamed x9 -> x12, local copies, waits for them, and re-layouts: 8.11 us -> 8.99 us
where the time goes in v2:
time: 134 us
  waiting for transfers between devices  65.1 us (49%)
  blocking collectives  21.7 us (16%)
  between operations  14.8 us (11%)
  local copies, waits for them, and re-layouts  10.9 us (8%)
  other arithmetic  9.06 us (7%)
  matrix products  8.51 us (6%)
  starting transfers between devices  3.61 us (3%)
    all_gather x1, waiting for transfers between devices, body(): updates = lax.all_gather(grouped, 'rep', axis=0, tiled=True)  49.5 us
    all_to_all x1, blocking collectives, body(): lax.all_to_all(outgoing, 'own', split_axis=0, concat_axis=1, tiled=True)  21.7 us
    all_to_all x1, waiting for transfers between devices, lanes_detail(): all_to_all(jnp.stack(jnp.split(view, axis_size('own'), axis=along_dim)),...  15.6 us
    unnamed x12, local copies, waits for them, and re-layouts  8.99 us
    dot_general x2, matrix products, orthogonalize(): jnp.dot(poly, iterate, preferred_element_type=jnp.float32)  5.42 us
    all_to_all x1, starting transfers between devices, lanes_detail(): all_to_all(jnp.stack(jnp.split(view, axis_size('own'), axis=along_dim)),...  3.56 us
    dot_general x2, matrix products, orthogonalize(): jnp.dot(iterate, iterate.T, preferred_element_type=jnp.float32)  3.1 us
  transfers between devices with their start and end apart: 2, of which 2 were waited for; matrix products, arithmetic and copies ran while one was open for 1% of the time, Pallas kernels for 0%

profile of v2, /device:TPU:0, one launch (start us, length us, event | category | flops | bytes accessed | tf_op | source)
XLA Modules:
  0.0 133.8 jit_solution(13756480437863896277)
XLA Ops:
  7.2 0.7 compare_convert_fusion
  7.9 0.7 fusion.18
  8.6 1.4 %convert_element_type.90 = bf16[4,72,1024]{2,1,0:T(8,128)(2,1)S(1)} convert(f32[4,72,1024]{2,1,0:T(8,128)} %param.3) | non-fusion elementwise | flops 294912 | bytes 1769472 | tf_op jit(solution)/shard_map/convert_element_type | solution.py:41
  10.7 21.7 %all_to_all.14 = bf16[8,72,1024]{2,1,0:T(8,128)(2,1)S(1)} all-to-all(bf16[8,72,1024]{2,1,0:T(8,128)(2,1)S(1)} %select_multiply_fusion), channel_id=1, replica_groups=mesh['rep'=4,'own'=8] {'own'}, dimensions={0} | all-to-all | bytes 2359296 | tf_op jit(solution)/shard_map/all_to_all | solution.py:43
  32.8 1.0 copy-done
  33.7 1.5 %convert_multiply_fusion = (f32[1,576,1024]{2,1,0:T(8,128)S(1)}, bf16[1,576,1024]{2,1,0:T(8,128)(2,1)}) fusion(bf16[1,576,1024]{2,1,0:T(8,128)(2,1)S(1)} %copy-done, f32[1,576,1024]{2,1,0:T(8,128)S(1)} %bitcast.74), kind=kLoop, calls=%fused_computation.13 | loop fusion | flops 2359296 | bytes 7077888 | tf_op jit(solution)/shard_map/mul | solution.py:45
  35.3 1.3 multiply_reduce_fusion
  37.7 2.0 %convolution_convert_fusion.1 = bf16[576,576]{1,0:T(8,128)(2,1)} fusion(bf16[576,1024]{1,0:T(8,128)(2,1)S(1)} %bitcast.76), kind=kOutput, calls=%fused_computation.19 | convolution fusion | flops 679809024 | bytes 1843200 | tf_op jit(solution)/shard_map/dot_general | solution.py:22
  40.3 3.6 %add_convert_fusion = bf16[576,1024]{1,0:T(8,128)(2,1)S(1)} fusion(bf16[576,1024]{1,0:T(8,128)(2,1)S(1)} %fusion.4, bf16[576,576]{1,0:T(8,128)(2,1)} %convolution_convert_fusion.1), kind=kOutput, calls=%fused_computation.9 | convolution fusion | flops 1065701376 | bytes 3022848 | tf_op jit(solution)/shard_map/dot_general | solution.py:25
  44.0 1.1 convolution_convert_fusion
  45.1 1.8 %fusion.5 = bf16[1,576,1024]{2,1,0:T(8,128)(2,1)S(1)} fusion(bf16[576,1024]{1,0:T(8,128)(2,1)S(1)} %add_convert_fusion, bf16[576,576]{1,0:T(8,128)(2,1)S(1)} %convolution_convert_fusion), kind=kOutput, calls=%fused_computation.17 | convolution fusion | flops 1066291200 | bytes 3022848 | tf_op jit(solution)/shard_map/dot_general | solution.py:25
  46.9 0.7 fusion.17
  47.5 0.7 fusion.16
  48.2 0.7 fusion.15
  48.9 0.7 fusion.14
  49.6 0.7 fusion.13
  50.2 0.7 fusion.12
  50.9 0.7 fusion.11
  52.3 3.6 %all-to-all-start.1 = ((bf16[8,1,72,1024]{3,2,1,0:T(8,128)(2,1)}), bf16[8,1,72,1024]{3,2,1,0:T(8,128)(2,1)S(1)}, u32[]{:S(2)}, u32[]{:S(2)}) async-start(bf16[8,1,72,1024]{3,2,1,0:T(8,128)(2,1)} %fusion.10), calls=%async_computation.1 | async-start | bytes 2359296 | tf_op jit(solution)/shard_map/all_to_all | solution.py:50
  55.9 1.0 sort.17
  56.9 15.6 %all-to-all-done.1 = bf16[8,1,72,1024]{3,2,1,0:T(8,128)(2,1)S(1)} async-done(((bf16[8,1,72,1024]{3,2,1,0:T(8,128)(2,1)}), bf16[8,1,72,1024]{3,2,1,0:T(8,128)(2,1)S(1)}, u32[]{:S(2)}, u32[]{:S(2)}) %all-to-all-start.1) | async-done | bytes 1179680 | tf_op jit(solution)/shard_map/all_to_all | solution.py:50
  73.1 0.9 broadcast_select_fusion
  74.1 49.5 %all-gather.2.cloned.1.call-done = bf16[16,72,1024]{2,1,0:T(8,128)(2,1)} async-done(((bf16[4,72,1024]{2,1,0:T(8,128)(2,1)}), bf16[16,72,1024]{2,1,0:T(8,128)(2,1)}) %all-gather.2.cloned.1.call-update) | async-done | bytes 2359312 | tf_op jit(solution)/shard_map/all_gather | solution.py:59
  123.6 3.3 %copy.13 = bf16[16,72,1024]{2,1,0:T(8,128)(2,1)} copy(bf16[16,72,1024]{2,1,0:T(8,128)(2,1)} %all-gather.2.cloned.1.call-done) | data formatting | bytes 4718592
  (17 shorter events, 3.5 us)
Async XLA Ops:
  32.5 1.3 copy-start
  37.7 2.0 %copy-start.1 = (bf16[1,576,1024]{2,1,0:T(8,128)(2,1)S(1)}, bf16[1,576,1024]{2,1,0:T(8,128)(2,1)}, u32[]{:S(2)}) copy-start(bf16[1,576,1024]{2,1,0:T(8,128)(2,1)} %param.4) | copy-start | bytes 3538948
  52.3 20.3 %all-to-all-start.1 = ((bf16[8,1,72,1024]{3,2,1,0:T(8,128)(2,1)}), bf16[8,1,72,1024]{3,2,1,0:T(8,128)(2,1)S(1)}, u32[]{:S(2)}, u32[]{:S(2)}) async-start(bf16[8,1,72,1024]{3,2,1,0:T(8,128)(2,1)} %fusion.10), calls=%async_computation.1 | async-start | bytes 2359296 | tf_op jit(solution)/shard_map/all_to_all | solution.py:50
  55.8 67.8 %all-gather.2.cloned.1.call-start = ((), (), s32[]{:S(2)}) async-start(), calls=%async_computation.2 | async-start | bytes 2949120 | tf_op jit(solution)/shard_map/all_gather | solution.py:59
Sparse Core Ops, SparseCore 0:
  74.2 49.3 all-gather.1
